TPU v7x, 32 devices: a whole 2x2x4 slice. The times are simulated.
32 devices in a mesh: row: 4 (over y, core), col: 8 (over z, x).
Axes of the slice: x: 2, y: 2, z: 4, core: 2. Of those that a mesh axis runs over, the one named last changes fastest.
Arguments:
- x_blocks: bfloat16 [4, 8, 21, 128, 128], P('row', 'col'), may hold values from -1.1953125 to 1.1953125
- x_slots: int32 [4, 8, 21], replicated, may hold values from 0 to 127, as said below
- x_count: int32 [4, 8], replicated, may hold values from 10 to 21, as said below
- s_slots: int32 [4, 8, 2], replicated, may hold values from 0 to 15, as said below
- s_count: int32 [4, 8], replicated, may hold values from 1 to 2, as said below
Outputs:
- square_blocks: bfloat16 [4, 8, 2, 128, 128], P('row', 'col')
- result_blocks: bfloat16 [4, 8, 2, 128, 128], P('row', 'col')
Inputs may be any that keep to these rules, and one draw needn't show every extreme that they name: `x_slots`: in each tile the live slots hold distinct positions; the live blocks whose position % 16 is below 2 come first among the live slots, at most 2 of them, and some tile has exactly 2. Positions of slots that are not live are arbitrary within the range. `x_count`: some tile has exactly 21 live slots. `s_slots`: in each tile the live slots hold distinct positions. `s_count`: some tile has exactly 2 live slots.
All inputs are finite; a program needn't handle non-finite values.
Results may differ from a plain program's by a relative error of at most 0.0049.
Values may be sent and summed in bfloat16 or wider, within the bound.
No kernel may reach another device: no remote copies, remote signals or barrier semaphores. Data moves between devices by JAX's collectives and lax.ppermute only.
A program may use at most 128 MiB of HBM per device.

v0:
```python
import math
import jax
import jax.numpy as jnp
from jax import lax
from jax.sharding import PartitionSpec as P

RB = 8
JW = 2
CAPW = 2


def match_index(targets, slot_keys, slot_live):
    matches = (targets[..., None] == slot_keys) & slot_live
    ordinal = jnp.arange(1, slot_keys.shape[0] + 1, dtype=jnp.int32)
    located = jnp.sum(jnp.where(matches, ordinal, 0), axis=-1)
    return jnp.where(located > 0, located - 1, slot_keys.shape[0])


def local(x_blocks, x_slots, x_count, s_slots, s_count):
    row_total = lax.axis_size("row")
    col_total = lax.axis_size("col")
    row_id = lax.axis_index("row")
    col_id = lax.axis_index("col")
    capacity = x_blocks.shape[2]
    block_size = x_blocks.shape[3]
    order_blocks = RB * col_total
    tile_width = order_blocks // row_total
    panel_all = lax.all_gather(x_blocks, "row", axis=0, tiled=True)
    stacked = panel_all.reshape(row_total * capacity, block_size, block_size)
    padded = jnp.concatenate(
        [stacked, jnp.zeros((1, block_size, block_size), stacked.dtype)], axis=0
    )
    column_slots = lax.dynamic_index_in_dim(x_slots, col_id, 1, keepdims=False)
    column_count = lax.dynamic_index_in_dim(x_count, col_id, 1, keepdims=False)
    ordinal = jnp.arange(capacity, dtype=jnp.int32)
    panel_live = (ordinal[None, :] < column_count[:, None]).reshape(-1)
    owners = jnp.arange(row_total, dtype=jnp.int32)[:, None]
    panel_keys = (
        column_slots // tile_width * order_blocks + owners * tile_width + column_slots % tile_width
    ).reshape(-1)
    row_lanes = jnp.arange(RB, dtype=jnp.int32)
    window_ids = jnp.arange(JW, dtype=jnp.int32)

    def accumulate(running, values, inner_row, inner_col, usable):
        picked = match_index(
            row_lanes[None, :] * order_blocks + inner_row[:, None], panel_keys, panel_live
        )
        left_part = jnp.take(padded, picked, axis=0)
        placing = ((inner_col[:, None] == window_ids[None, :]) & usable[:, None]).astype(
            values.dtype
        )
        placed = placing[:, :, None, None] * values[:, None, :, :]
        return running + jnp.einsum(
            "nrxy,njyz->rjxz", left_part, placed, preferred_element_type=jnp.float32
        )

    def make_step(slot_table, count_row, stride, column_limit):

        def fold_step(running, piece, offset):
            pieces = piece.shape[1]
            slot_count = piece.shape[2]
            positions = lax.dynamic_slice_in_dim(slot_table, offset, pieces, 0)[:, :slot_count]
            counts = lax.dynamic_slice_in_dim(count_row, offset, pieces, 0)
            owner_ids = offset + jnp.arange(pieces, dtype=jnp.int32)[:, None]
            inner_row = owner_ids * RB + positions // stride
            inner_col = positions % stride
            usable = (jnp.arange(slot_count, dtype=jnp.int32)[None, :] < counts[:, None]) & (
                inner_col < column_limit
            )
            values = piece.reshape(pieces * slot_count, block_size, block_size)
            return accumulate(
                running, values, inner_row.reshape(-1), inner_col.reshape(-1), usable.reshape(-1)
            )

        return fold_step

    blank_sum = jnp.zeros((RB, JW, block_size, block_size), jnp.float32)

    def collect_all(gathered, fold_step):
        per_turn = math.gcd(col_total, 8)

        def advance(turn_index, running):
            offset = turn_index * per_turn
            portion = lax.dynamic_slice_in_dim(gathered, offset, per_turn, 1)
            return fold_step(running, portion, offset)

        return lax.fori_loop(0, col_total // per_turn, advance, blank_sum)

    row_slots = lax.dynamic_index_in_dim(x_slots, row_id, 0, keepdims=False)
    row_count = lax.dynamic_index_in_dim(x_count, row_id, 0, keepdims=False)
    square_slots = lax.dynamic_index_in_dim(s_slots, row_id, 0, keepdims=False)
    square_count = lax.dynamic_index_in_dim(s_count, row_id, 0, keepdims=False)
    window_part = x_blocks[:, :, :CAPW]
    first_step = make_step(row_slots, row_count, tile_width, JW)
    product = collect_all(lax.all_gather(window_part, "col", axis=1, tiled=True), first_step)
    own_slots = lax.dynamic_index_in_dim(square_slots, col_id, 0, keepdims=False)
    own_count = lax.dynamic_index_in_dim(square_count, col_id, 0, keepdims=False)
    own_live = jnp.arange(own_slots.shape[0], dtype=jnp.int32) < own_count
    flat_one = product.reshape(RB * JW, block_size, block_size)
    square_part = jnp.where(
        own_live[:, None, None], jnp.take(flat_one, own_slots, axis=0), 0.0
    ).astype(jnp.bfloat16)
    square_part = square_part[None, None]
    second_step = make_step(square_slots, square_count, JW, JW)
    second = collect_all(lax.all_gather(square_part, "col", axis=1, tiled=True), second_step)
    own_keys = own_slots // JW * order_blocks + row_id * tile_width + own_slots % JW
    own_block = jnp.take(padded, match_index(own_keys, panel_keys, panel_live), axis=0).astype(
        jnp.float32
    )
    flat_two = second.reshape(RB * JW, block_size, block_size)
    combined = 1.5 * own_block - 0.5 * jnp.take(flat_two, own_slots, axis=0)
    result = jnp.where(own_live[:, None, None], combined, 0.0).astype(jnp.bfloat16)
    return (square_part, result[None, None])


def solution(mesh):
    in_specs = (P("row", "col", None, None, None), P(), P(), P(), P())
    out_specs = (P("row", "col", None, None, None), P("row", "col", None, None, None))
    return jax.shard_map(local, mesh=mesh, in_specs=in_specs, out_specs=out_specs, check_vma=False)
```

profile of v0, /device:TPU:0, one launch (start us, length us, event | category | flops | bytes accessed | tf_op | source)
XLA Modules:
  0.0 114.3 jit_solution(4241437289012086558)
XLA Ops:
  7.2 0.0 copy-start
  7.2 0.0 all-gather.3.cloned.1.call-start
  7.2 0.7 all-gather.3.cloned.1.call-update
  7.9 0.0 copy-done
  8.0 0.9 dynamic-slice_reduce_fusion
  8.9 0.7 fusion.33
  9.6 0.7 constant_dynamic-slice_fusion.1
  10.2 0.9 fusion.30
  11.1 1.3 %dynamic_slice.43 = s32[1,1]{1,0:T(1,128)} dynamic-slice(s32[4,8]{1,0:T(4,128)} %param.13, s32[]{:T(128)S(6)} %select_n.191, s32[]{:T(128)S(6)} %select_n.193), dynamic_slice_sizes={1,1} | dynamic-slice | bytes 12 | tf_op jit(solution)/shard_map/jit(dynamic_index_in_dim)/dynamic_slice | solution.py:97
  12.4 0.1 fusion.26
  12.5 0.1 fusion.25
  12.5 0.1 add.297
  12.6 0.1 copy.31
  12.7 0.1 squeeze.29
  12.8 0.1 add.295
  12.8 0.1 add.313
  12.9 0.1 squeeze.27
  13.0 0.1 add.300
  13.1 0.1 add.301
  13.2 0.1 iota_compare_fusion.2
  13.2 0.1 lt.193
  13.4 0.1 broadcast_add_fusion.1
  13.4 0.7 select_reduce_fusion
  14.1 0.1 reshape.561
  14.2 0.1 and.203
  14.3 0.1 eq.110
  14.4 0.9 slice.19
  15.3 33.1 %all_gather.9 = bf16[1,8,2,128,128]{4,3,2,0,1:T(8,128)(2,1)S(1)} all-gather(bf16[1,1,2,128,128]{4,3,2,0,1:T(8,128)(2,1)S(1)} %slice.19), channel_id=1, replica_groups=mesh['row'=4,'col'=8] {'col'}, dimensions={1}, use_global_device_ids=true | all-gather | bytes 589824 | tf_op jit(solution)/shard_map/all_gather | solution.py:95
  48.4 0.3 copy.28
  48.7 0.1 reshape.567
  48.8 0.1 iota_compare_fusion
  48.9 0.1 lt.202
  49.0 0.2 fusion.29
  49.2 0.7 compare_and_fusion.2
  50.0 0.0 all-gather.3.cloned.1.call-done
  50.0 2.0 %concatenate.3 = bf16[85,128,128]{2,1,0:T(8,128)(2,1)S(1)} pad(bf16[84,128,128]{2,1,0:T(8,128)(2,1)} %bitcast.54, bf16[]{:T(256)} %constant.234.clone.1), padding=0_1x0_0x0_0 | pad | bytes 5537794 | tf_op jit(solution)/shard_map/concatenate | solution.py:30
  52.0 3.0 %gather_fusion.1 = bf16[128,128,128]{2,1,0:T(8,128)(2,1)} fusion(bf16[85,128,128]{2,1,0:T(8,128)(2,1)S(1)} %concatenate.3, s32[1024]{0:T(1024)S(1)} %pad_clamp_fusion.3), kind=kCustom, calls=%fused_computation.clone | custom fusion | bytes 8389120 | tf_op jit(solution)/shard_map/while/body/eval_jaxpr/jit(_take)/gather | solution.py:48
  55.0 4.4 %fusion.6 = bf16[8,2,128,128]{2,3,0,1:T(8,128)(2,1)} fusion(bf16[16,128,128]{1,2,0:T(8,128)(2,1)S(1)} %copy.28, bf16[16,2]{0,1:T(2,128)(2,1)S(1)} %and_convert_fusion.1, bf16[16,8,128,128]{3,2,1,0:T(8,128)(2,1)} %bitcast.52, pred[16,8]{1,0:T(8,128)(4,1)S(1)} %compare_and_fusion.1), kind=kOutput, calls=%fused_computation.13 | convolution fusion | flops 1077936128 | bytes 5243072 | tf_op jit(solution)/shard_map/while/body/eval_jaxpr/nrxy,njyz->rjxz/dot_general | solution.py:53
  59.3 1.3 %copy.30 = bf16[8,2,128,128]{3,2,1,0:T(8,128)(2,1)S(1)} copy(bf16[8,2,128,128]{2,3,0,1:T(8,128)(2,1)} %fusion.6) | data formatting | bytes 1048576 | tf_op jit(solution)/shard_map/while/body/eval_jaxpr/nrxy,njyz->rjxz/transpose | solution.py:53
  60.7 0.6 gather_fusion.2
  61.2 0.1 fusion.23
  61.3 0.7 fusion.37
  62.0 31.2 %all-gather = bf16[16,128,128]{2,1,0:T(8,128)(2,1)S(1)} all-gather(bf16[2,128,128]{2,1,0:T(8,128)(2,1)S(1)} %fusion.23), channel_id=2, replica_groups=mesh['row'=4,'col'=8] {'col'}, dimensions={0}, use_global_device_ids=true | all-gather | bytes 589824 | tf_op jit(solution)/shard_map/all_gather | solution.py:105
  93.3 1.0 copy.32
  94.3 0.0 copy-start.1
  94.3 3.0 %gather_fusion.3 = bf16[128,128,128]{2,1,0:T(8,128)(2,1)} fusion(bf16[85,128,128]{2,1,0:T(8,128)(2,1)S(1)} %concatenate.3, s32[1024]{0:T(1024)S(1)} %pad_clamp_fusion), kind=kCustom, calls=%fused_computation.2.clone | custom fusion | bytes 8389120 | tf_op jit(solution)/shard_map/while/body/eval_jaxpr/jit(_take)/gather | solution.py:48
  97.3 0.0 copy-done.1
  97.3 4.5 %fusion.9 = f32[8,2,128,128]{2,3,0,1:T(8,128)} fusion(bf16[16,128,128]{1,2,0:T(8,128)(2,1)S(1)} %copy-done.1, bf16[16,2]{0,1:T(2,128)(2,1)S(1)} %and_convert_fusion, bf16[16,8,128,128]{3,2,1,0:T(8,128)(2,1)} %bitcast.53, pred[16,8]{1,0:T(8,128)(4,1)S(1)} %compare_and_fusion), kind=kOutput, calls=%fused_computation.14 | convolution fusion | flops 1077936128 | bytes 5767360 | tf_op jit(solution)/shard_map/while/body/eval_jaxpr/nrxy,njyz->rjxz/dot_general | solution.py:53
  101.8 2.5 %copy.34 = f32[8,2,128,128]{3,2,1,0:T(8,128)} copy(f32[8,2,128,128]{2,3,0,1:T(8,128)} %fusion.9) | data formatting | bytes 2097152 | tf_op jit(solution)/shard_map/while/body/eval_jaxpr/nrxy,njyz->rjxz/transpose | solution.py:53
  104.3 1.8 %gather_fusion.4 = f32[2,128,128]{2,1,0:T(8,128)S(1)} fusion(f32[16,128,128]{2,1,0:T(8,128)} %bitcast.56, s32[1024]{0:T(1024)S(1)} %pad_clamp_fusion.2), kind=kCustom, calls=%fused_computation.3.clone | custom fusion | bytes 262152 | tf_op jit(solution)/shard_map/jit(_take)/gather | solution.py:111
  106.1 0.6 gather_fusion
  106.7 0.7 fusion.24
  (21 shorter events, 0.2 us)
Async XLA Ops:
  7.2 0.8 copy-start
  7.2 42.8 %all-gather.3.cloned.1.call-start = ((), (), s32[]{:S(2)}) async-start(), calls=%async_computation | async-start | bytes 3440640 | tf_op jit(solution)/shard_map/all_gather | solution.py:28
  94.3 3.0 %copy-start.1 = (bf16[16,128,128]{1,2,0:T(8,128)(2,1)S(1)}, bf16[16,128,128]{1,2,0:T(8,128)(2,1)}, u32[]{:S(2)}) copy-start(bf16[16,128,128]{1,2,0:T(8,128)(2,1)} %copy.32) | copy-start | bytes 1572868
Sparse Core Ops, SparseCore 0:
  9.5 28.9 all-gather.2
where the time goes:
time: 115 us; the launch traced here: 114 us
  blocking collectives  64.4 us (56%)
  local copies, waits for them, and re-layouts  22.5 us (20%)
  between operations  14.2 us (12%)
  matrix products  8.87 us (8%)
  other arithmetic  3.59 us (3%)
    all_gather x1, blocking collectives, local(): lax.all_gather(window_part, 'col', axis=1, tiled=True)  33.1 us
    all_gather x1, blocking collectives, local(): lax.all_gather(square_part, 'col', axis=1, tiled=True)  31.2 us
    dot_general x2, matrix products, accumulate(): jnp.einsum('nrxy,njyz->rjxz', left_part, placed, preferred_element_type=j...  8.87 us
    gather x2, local copies, waits for them, and re-layouts, accumulate(): left_part = jnp.take(padded, picked, axis=0)  6.02 us
    transpose x2, local copies, waits for them, and re-layouts, accumulate(): jnp.einsum('nrxy,njyz->rjxz', left_part, placed, preferred_element_type=j...  3.86 us
  transfers between devices with their start and end apart: 1, of which 0 were waited for; matrix products, arithmetic and copies ran while one was open for 8% of the time, Pallas kernels for 0%

commit v1 on v0

--- a/solution.py
+++ b/solution.py
@@ -7,6 +7,13 @@
 RB = 8
 JW = 2
 CAPW = 2
+
+
+def swapped_in(shard, axis, along):
+    size = lax.axis_size(axis)
+    blocks = jnp.stack([shard for _ in range(size)])
+    blocks = lax.all_to_all(blocks, axis, split_axis=0, concat_axis=0)
+    return jnp.concatenate(blocks, axis=along)
 
 
 def match_index(targets, slot_keys, slot_live):
@@ -102,7 +109,7 @@
     ).astype(jnp.bfloat16)
     square_part = square_part[None, None]
     second_step = make_step(square_slots, square_count, JW, JW)
-    second = collect_all(lax.all_gather(square_part, "col", axis=1, tiled=True), second_step)
+    second = collect_all(swapped_in(square_part, "col", 1), second_step)
     own_keys = own_slots // JW * order_blocks + row_id * tile_width + own_slots % JW
     own_block = jnp.take(padded, match_index(own_keys, panel_keys, panel_live), axis=0).astype(
         jnp.float32

time: 115 us -> 90.3 us (0.79)
  blocking collectives: 64.4 us -> 33.1 us
  waiting for transfers between devices: 0.7 us -> 6.55 us
  starting transfers between devices: 0.04 us -> 5.55 us
  local copies, waits for them, and re-layouts: 22.5 us -> 19.1 us
  matrix products: 8.87 us -> 7.63 us
    all_gather x1 -> x0, blocking collectives: 31.2 us -> none  [local(): lax.all_gather(square_part, 'col', axis=1, tiled=True)]
    all_to_all x0 -> x1, waiting for transfers between devices: none -> 5.85 us  [swapped_in(): blocks = lax.all_to_all(blocks, axis, split_axis=0, concat_axis=0)]
    all_to_all x0 -> x1, starting transfers between devices: none -> 5.51 us  [swapped_in(): blocks = lax.all_to_all(blocks, axis, split_axis=0, concat_axis=0)]
    transpose x2, local copies, waits for them, and re-layouts: 3.86 us -> 1.64 us  [accumulate(): jnp.einsum('nrxy,njyz->rjxz', left_part, placed, preferred_element_type=j...]
    dot_general x2, matrix products: 8.87 us -> 7.63 us  [accumulate(): jnp.einsum('nrxy,njyz->rjxz', left_part, placed, preferred_element_type=j...]
    gather x1, local copies, waits for them, and re-layouts: 1.78 us -> 0.56 us  [local(): combined = 1.5 * own_block - 0.5 * jnp.take(flat_two, own_slots, axis=0)]
  transfers between devices with their start and end apart: 1 -> 2, of which waited for: 0 -> 1; matrix products, arithmetic and copies ran while one was open for 8% -> 15% of each run, Pallas kernels for 0% -> 0%
where the time goes in v1:
time: 90.3 us; the launch traced here: 89.8 us
  blocking collectives  33.1 us (37%)
  local copies, waits for them, and re-layouts  19.1 us (21%)
  between operations  14.2 us (16%)
  matrix products  7.63 us (8%)
  waiting for transfers between devices  6.55 us (7%)
  starting transfers between devices  5.55 us (6%)
  other arithmetic  3.59 us (4%)
    all_gather x1, blocking collectives, local(): lax.all_gather(window_part, 'col', axis=1, tiled=True)  33.1 us
    dot_general x2, matrix products, accumulate(): jnp.einsum('nrxy,njyz->rjxz', left_part, placed, preferred_element_type=j...  7.63 us
    gather x2, local copies, waits for them, and re-layouts, accumulate(): left_part = jnp.take(padded, picked, axis=0)  6.02 us
    all_to_all x1, waiting for transfers between devices, swapped_in(): blocks = lax.all_to_all(blocks, axis, split_axis=0, concat_axis=0)  5.85 us
    all_to_all x1, starting transfers between devices, swapped_in(): blocks = lax.all_to_all(blocks, axis, split_axis=0, concat_axis=0)  5.51 us
    concatenate x1, local copies, waits for them, and re-layouts, local(): jnp.concatenate([stacked, jnp.zeros((1, block_size, block_size), stacked....  1.97 us
  transfers between devices with their start and end apart: 2, of which 1 were waited for; matrix products, arithmetic and copies ran while one was open for 15% of the time, Pallas kernels for 0%

profile of v1, /device:TPU:0, one launch (start us, length us, event | category | flops | bytes accessed | tf_op | source)
XLA Modules:
  0.0 89.8 jit_solution(16559252481376220606)
XLA Ops:
  7.2 0.0 copy-start
  7.2 0.0 all-gather.2.cloned.1.call-start
  7.2 0.7 all-gather.2.cloned.1.call-update
  7.9 0.0 copy-done
  8.0 0.7 fusion.33
  8.7 0.1 fusion.26
  8.7 0.1 fusion.25
  8.8 0.1 add.297
  8.9 0.9 dynamic-slice_reduce_fusion
  9.8 1.3 %dynamic_slice.43 = s32[1,1]{1,0:T(1,128)} dynamic-slice(s32[4,8]{1,0:T(4,128)} %param.13, s32[]{:T(128)S(6)} %select_n.191, s32[]{:T(128)S(6)} %select_n.193), dynamic_slice_sizes={1,1} | dynamic-slice | bytes 12 | tf_op jit(solution)/shard_map/jit(dynamic_index_in_dim)/dynamic_slice | solution.py:104
  11.0 0.9 fusion.30
  11.9 0.7 constant_dynamic-slice_fusion.1
  12.6 0.1 copy.31
  12.7 0.1 squeeze.29
  12.7 0.1 add.295
  12.8 0.1 add.313
  12.9 0.1 squeeze.27
  13.0 0.1 add.300
  13.1 0.1 add.301
  13.2 0.1 iota_compare_fusion.2
  13.3 0.1 lt.193
  13.4 0.1 broadcast_add_fusion.1
  13.5 0.7 select_reduce_fusion
  14.2 0.1 reshape.563
  14.2 0.1 and.203
  14.3 0.1 eq.110
  14.4 0.9 slice.19
  15.3 33.1 %all_gather.6 = bf16[1,8,2,128,128]{4,3,2,0,1:T(8,128)(2,1)S(1)} all-gather(bf16[1,1,2,128,128]{4,3,2,0,1:T(8,128)(2,1)S(1)} %slice.19), channel_id=1, replica_groups=mesh['row'=4,'col'=8] {'col'}, dimensions={1}, use_global_device_ids=true | all-gather | bytes 589824 | tf_op jit(solution)/shard_map/all_gather | solution.py:102
  48.4 0.3 copy.28
  48.7 0.1 reshape.569
  48.8 0.7 iota_compare_fusion.3
  49.5 0.2 fusion.29
  49.7 0.1 iota_compare_fusion
  49.8 0.0 all-gather.2.cloned.1.call-done
  49.9 2.0 %concatenate.3 = bf16[85,128,128]{2,1,0:T(8,128)(2,1)S(1)} pad(bf16[84,128,128]{2,1,0:T(8,128)(2,1)} %bitcast.55, bf16[]{:T(256)} %constant.234.clone.1), padding=0_1x0_0x0_0 | pad | bytes 5537794 | tf_op jit(solution)/shard_map/concatenate | solution.py:37
  51.8 3.0 %gather_fusion.1 = bf16[128,128,128]{2,1,0:T(8,128)(2,1)} fusion(bf16[85,128,128]{2,1,0:T(8,128)(2,1)S(1)} %concatenate.3, s32[1024]{0:T(1024)S(1)} %pad_clamp_fusion.3), kind=kCustom, calls=%fused_computation.clone | custom fusion | bytes 8389120 | tf_op jit(solution)/shard_map/while/body/eval_jaxpr/jit(_take)/gather | solution.py:55
  54.8 4.3 %fusion.6 = bf16[8,2,128,128]{2,3,0,1:T(8,128)(2,1)} fusion(bf16[16,128,128]{1,2,0:T(8,128)(2,1)S(1)} %copy.28, bf16[16,2]{0,1:T(2,128)(2,1)S(1)} %and_convert_fusion.1, bf16[16,8,128,128]{3,2,1,0:T(8,128)(2,1)} %bitcast.54, pred[16,8]{1,0:T(8,128)(4,1)S(1)} %compare_and_fusion.1), kind=kOutput, calls=%fused_computation.13 | convolution fusion | flops 1077936128 | bytes 5243072 | tf_op jit(solution)/shard_map/while/body/eval_jaxpr/nrxy,njyz->rjxz/dot_general | solution.py:60
  59.2 1.3 %copy.30 = bf16[8,2,128,128]{3,2,1,0:T(8,128)(2,1)S(1)} copy(bf16[8,2,128,128]{2,3,0,1:T(8,128)(2,1)} %fusion.6) | data formatting | bytes 1048576 | tf_op jit(solution)/shard_map/while/body/eval_jaxpr/nrxy,njyz->rjxz/transpose | solution.py:60
  60.5 0.6 gather_fusion.2
  61.1 0.1 fusion.23
  61.2 0.1 copy.32
  61.3 0.9 %stack.3 = bf16[8,1,1,2,128,128]{4,5,3,2,1,0:T(8,128)(2,1)} broadcast(bf16[2,128,128]{1,2,0:T(8,128)(2,1)S(1)} %copy.32), dimensions={3,4,5} | broadcast | bytes 589824 | tf_op jit(solution)/shard_map/stack | solution.py:14
  62.2 5.5 %all-to-all-start = ((bf16[8,1,1,2,128,128]{4,5,3,2,1,0:T(8,128)(2,1)}), bf16[8,1,1,2,128,128]{4,5,3,2,1,0:T(8,128)(2,1)S(1)}, u32[]{:S(2)}, u32[]{:S(2)}) async-start(bf16[8,1,1,2,128,128]{4,5,3,2,1,0:T(8,128)(2,1)} %stack.3), calls=%async_computation | async-start | bytes 1048576 | tf_op jit(solution)/shard_map/all_to_all | solution.py:15
  67.7 0.1 lt.202
  67.8 3.0 %gather_fusion.3 = bf16[128,128,128]{2,1,0:T(8,128)(2,1)} fusion(bf16[85,128,128]{2,1,0:T(8,128)(2,1)S(1)} %concatenate.3, s32[1024]{0:T(1024)S(1)} %pad_clamp_fusion), kind=kCustom, calls=%fused_computation.2.clone | custom fusion | bytes 8389120 | tf_op jit(solution)/shard_map/while/body/eval_jaxpr/jit(_take)/gather | solution.py:55
  70.9 0.6 gather_fusion
  71.4 0.7 fusion.37
  72.1 5.8 %all-to-all-done = bf16[8,1,1,2,128,128]{4,5,3,2,1,0:T(8,128)(2,1)S(1)} async-done(((bf16[8,1,1,2,128,128]{4,5,3,2,1,0:T(8,128)(2,1)}), bf16[8,1,1,2,128,128]{4,5,3,2,1,0:T(8,128)(2,1)S(1)}, u32[]{:S(2)}, u32[]{:S(2)}) %all-to-all-start) | async-done | bytes 524320 | tf_op jit(solution)/shard_map/all_to_all | solution.py:15
  78.0 3.3 %fusion.9 = f32[8,2,128,128]{2,3,0,1:T(8,128)S(1)} fusion(bf16[16,128,128]{1,2,0:T(8,128)(2,1)S(1)} %bitcast.60, bf16[16,2]{0,1:T(2,128)(2,1)S(1)} %and_convert_fusion, bf16[16,8,128,128]{3,2,1,0:T(8,128)(2,1)} %bitcast.53, pred[16,8]{1,0:T(8,128)(4,1)S(1)} %compare_and_fusion), kind=kOutput, calls=%fused_computation.14 | convolution fusion | flops 1077936128 | bytes 5767360 | tf_op jit(solution)/shard_map/while/body/eval_jaxpr/nrxy,njyz->rjxz/dot_general | solution.py:60
  81.3 0.3 copy.34
  81.6 0.6 gather_fusion.4
  82.2 0.7 fusion.24
  (22 shorter events, 0.2 us)
Async XLA Ops:
  7.2 0.8 copy-start
  7.2 42.7 %all-gather.2.cloned.1.call-start = ((), (), s32[]{:S(2)}) async-start(), calls=%async_computation.1 | async-start | bytes 3440640 | tf_op jit(solution)/shard_map/all_gather | solution.py:35
  62.2 15.8 %all-to-all-start = ((bf16[8,1,1,2,128,128]{4,5,3,2,1,0:T(8,128)(2,1)}), bf16[8,1,1,2,128,128]{4,5,3,2,1,0:T(8,128)(2,1)S(1)}, u32[]{:S(2)}, u32[]{:S(2)}) async-start(bf16[8,1,1,2,128,128]{4,5,3,2,1,0:T(8,128)(2,1)} %stack.3), calls=%async_computation | async-start | bytes 1048576 | tf_op jit(solution)/shard_map/all_to_all | solution.py:15
Sparse Core Ops, SparseCore 0:
  9.5 28.9 all-gather.1
